TPU v7x, 32 devices: a whole 2x2x4 slice. The times are simulated.
32 devices in a mesh: dp: 8 (over z, y), expert: 2 (over core), tensor: 2 (over x).
Axes of the slice: x: 2, y: 2, z: 4, core: 2. Of those that a mesh axis runs over, the one named last changes fastest.
Arguments:
- dense_act: bfloat16 [2, 32, 512, 3584], P(None, 'dp', 'expert', 'tensor'), may hold values from -6 to 6
- dense_cot: bfloat16 [2, 32, 512, 3584], P(None, 'dp', ('expert', 'tensor')), may hold values from -6 to 6
- dense_proj_in: bfloat16 [2, 3584, 128], P(None, 'tensor'), may hold values from -0.09375 to 0.09375
- dense_proj_out: bfloat16 [2, 3584, 128], replicated, may hold values from -0.09375 to 0.09375
- expert_act: bfloat16 [32, 8, 64, 2560], P('dp', 'expert', None, 'tensor'), may hold values from -6 to 6
- expert_cot: bfloat16 [32, 8, 64, 3584], P('dp', 'expert', 'tensor'), may hold values from -6 to 6
- expert_proj_in: bfloat16 [2560, 128], P('tensor'), may hold values from -0.125 to 0.125
- expert_proj_out: bfloat16 [3584, 128], replicated, may hold values from -0.09375 to 0.09375
- dense_valid: float32 [2, 128, 128], replicated, may hold values from -0.0012207031 to 0.0012207031
- expert_valid: float32 [8, 128, 128], P('expert'), may hold values from -0.0012207031 to 0.0012207031
- domain_ids: int32 [32], P('dp'), may hold values from 0 to 63
- prior_mix: float32 [64], replicated, may hold values from 0.002 to 0.05
Outputs:
- log_mixture_weights: float32 [64], P('dp')
All inputs are finite; a program needn't handle non-finite values.
Results may differ from a plain program's by a relative error of at most 0.0003.
Values sent between devices are 32-bit elements; how exact they have to be, the bound alone decides.
A program may use at most 128 MiB of HBM per device.

v0:
```python
import jax
import jax.numpy as jnp
from jax import lax
from jax.sharding import PartitionSpec as P


def per_device(
    dense_act,
    dense_cot,
    dense_proj_in,
    dense_proj_out,
    expert_act,
    expert_cot,
    expert_proj_in,
    expert_proj_out,
    dense_valid,
    expert_valid,
    domain_ids,
    prior_mix,
):
    block = dense_act
    dense_update_vector = lax.psum_scatter(
        jnp.einsum("lmtd,ldr->tlmr", block, dense_proj_in, preferred_element_type=jnp.float32),
        "tensor",
        scatter_dimension=0,
        tiled=True,
    )
    dense_weight_matrix = jnp.einsum(
        "lmtd,ldr->tlmr", dense_cot, dense_proj_out, preferred_element_type=jnp.float32
    )
    dense_portion = jnp.einsum(
        "fquy,fquh->quyh", dense_update_vector, dense_weight_matrix, precision=lax.Precision.HIGHEST
    )
    block = expert_act
    expert_u = lax.psum_scatter(
        jnp.einsum("mecf,fr->cmer", block, expert_proj_in, preferred_element_type=jnp.float32),
        "tensor",
        scatter_dimension=0,
        tiled=True,
    )
    expert_weight_matrix = jnp.einsum(
        "mecd,dr->cmer", expert_cot, expert_proj_out, preferred_element_type=jnp.float32
    )
    expert_part = jnp.einsum(
        "cmer,cmes->mers", expert_u, expert_weight_matrix, precision=lax.Precision.HIGHEST
    )
    dense_full = lax.psum(dense_portion, ("expert", "tensor"))
    dense_score = jnp.sum(dense_full * dense_valid[:, None], axis=(0, 2, 3))
    expert_full = lax.psum(expert_part, "tensor")
    expert_local = jnp.sum(expert_full * expert_valid[None], axis=(1, 2, 3))
    score = dense_score + lax.psum(expert_local, "expert")
    domains = prior_mix.shape[0]
    onehot = (domain_ids[:, None] == jnp.arange(domains, dtype=jnp.int32)[None, :]).astype(
        jnp.float32
    )
    domain_part = jnp.dot(score, onehot, precision=lax.Precision.HIGHEST)
    share_tally_count = domains // lax.axis_size("dp")
    first_domain = lax.axis_index("dp") * share_tally_count
    previous_domain_share = lax.dynamic_slice_in_dim(prior_mix, first_domain, share_tally_count, 0)
    domain_total = lax.psum(domain_part, "dp")
    spread = jnp.sqrt(jnp.mean(domain_total * domain_total) + 1e-06)
    z_value = domain_total / spread
    mass = jnp.sum(prior_mix * jnp.exp(0.5 * z_value))
    z_share = lax.dynamic_slice_in_dim(z_value, first_domain, share_tally_count, 0)
    return jnp.log(previous_domain_share) + 0.5 * z_share - jnp.log(mass)


def solution(mesh):
    placed = (
        P(None, "dp", "expert", "tensor"),
        P(None, "dp", ("expert", "tensor"), None),
        P(None, "tensor", None),
        P(),
        P("dp", "expert", None, "tensor"),
        P("dp", "expert", "tensor", None),
        P("tensor", None),
        P(),
        P(),
        P("expert", None, None),
        P("dp"),
        P(),
    )
    return jax.shard_map(per_device, mesh=mesh, in_specs=placed, out_specs=P("dp"), check_vma=False)
```

profile of v0, /device:TPU:0, one launch (start us, length us, event | category | flops | bytes accessed | tf_op | source)
XLA Modules:
  0.0 206.4 jit_solution(693878961875852554)
XLA Ops:
  6.5 1.7 copy-done
  8.3 1.8 convolution_bitcast_fusion.1
  10.1 1.1 copy.18
  11.3 5.6 %convolution_bitcast_fusion = f32[256,2,4,128]{0,3,2,1:T(8,128)S(1)} fusion(bf16[2,4,256,1792]{3,2,1,0:T(8,128)(2,1)} %param.12, bf16[2,1792,128]{2,1,0:T(8,128)(2,1)S(1)} %copy-done.3), kind=kOutput, calls=%fused_computation.2 | convolution fusion | flops 939524096 | bytes 9306112 | tf_op jit(solution)/shard_map/lmtd,ldr->tlmr/dot_general | solution.py:23
  16.9 26.2 %copy.29 = f32[256,2,4,128]{2,3,1,0:T(8,128)} copy(f32[256,2,4,128]{0,3,2,1:T(8,128)S(1)} %convolution_bitcast_fusion) | data formatting | bytes 2097152
  43.2 29.4 %reshape.9 = f32[256,1024]{1,0:T(8,128)} reshape(f32[256,2,128,4]{3,2,1,0:T(8,128)} %bitcast.46) | data formatting | bytes 2097152
  72.6 0.6 dynamic-slice
  73.9 3.3 %fusion.6 = f32[128,4,4,32]{0,3,2,1:T(8,128)S(1)} fusion(bf16[4,4,32,3584]{3,2,1,0:T(8,128)(2,1)} %param.17, bf16[3584,128]{1,0:T(8,128)(2,1)S(1)} %copy-done.7), kind=kOutput, calls=%fused_computation.8 | convolution fusion | flops 469762048 | bytes 4849664 | tf_op jit(solution)/shard_map/mecd,dr->cmer/dot_general | solution.py:41
  77.2 1.0 constant_dynamic-slice_fusion
  78.2 2.8 %fusion.9 = f32[4,4,128,128]{3,2,1,0:T(8,128)} fusion(f32[128,4,4,32]{0,3,2,1:T(8,128)S(1)} %fusion.6, f32[32,4,4,128]{3,2,1,0:T(4,128)S(1)} %constant_dynamic-slice_fusion), kind=kOutput, calls=%fused_computation.12 | convolution fusion | flops 100663296 | bytes 1572864 | tf_op jit(solution)/shard_map/cmer,cmes->mers/dot_general | solution.py:44
  81.3 5.6 %fusion.2 = f32[128,2,4,128]{0,3,2,1:T(8,128)S(1)} fusion(bf16[2,4,128,3584]{3,2,1,0:T(8,128)(2,1)} %param.13, bf16[2,3584,128]{2,1,0:T(8,128)(2,1)S(1)} %copy-done.2), kind=kOutput, calls=%fused_computation.3 | convolution fusion | flops 939524096 | bytes 9699328 | tf_op jit(solution)/shard_map/lmtd,ldr->tlmr/dot_general | solution.py:28
  86.9 8.9 %reduce-scatter.4.cloned.1.call-done = f32[128,1024]{1,0:T(8,128)} async-done(((f32[256,1024]{1,0:T(8,128)}), f32[128,1024]{1,0:T(8,128)}) %reduce-scatter.4.cloned.1.call-update) | async-done | bytes 524304
  95.8 19.5 %reshape.10 = f32[128,2,128,4]{3,2,1,0:T(8,128)} reshape(f32[128,1024]{1,0:T(8,128)} %reduce-scatter.4.cloned.1.call-done) | data formatting | bytes 1048576
  115.3 13.2 %copy.16 = f32[128,2,4,128]{0,3,2,1:T(8,128)} copy(f32[128,2,4,128]{2,3,1,0:T(8,128)} %bitcast.47) | data formatting | bytes 1048576 | tf_op jit(solution)/shard_map/reduce_scatter | solution.py:22
  128.5 3.1 %fusion.12 = f32[2,4,128,128]{3,2,1,0:T(8,128)} fusion(f32[128,2,4,128]{0,3,2,1:T(8,128)} %copy.16, f32[128,2,4,128]{0,3,2,1:T(8,128)S(1)} %fusion.2), kind=kOutput, calls=%fused_computation.22 | convolution fusion | flops 201326592 | bytes 1572864 | tf_op jit(solution)/shard_map/fquy,fquh->quyh/dot_general | solution.py:31
  131.6 6.7 %all-reduce.7.cloned.1.call-done = f32[4,4,128,128]{3,2,1,0:T(8,128)} async-done(((f32[4,4,128,128]{3,2,1,0:T(8,128)}), f32[4,4,128,128]{3,2,1,0:T(8,128)}) %all-reduce.7.cloned.1.call-update) | async-done | bytes 1048592 | tf_op jit(solution)/shard_map/psum | solution.py:49
  138.3 1.4 multiply_reduce_fusion
  139.7 2.4 %psum.30 = f32[4]{0:T(128)S(1)} all-reduce(f32[4]{0:T(128)S(1)} %multiply_reduce_fusion), channel_id=1, replica_groups=mesh['dp'=8,'expert'=2,'tensor'=2] {'expert'}, use_global_device_ids=true, to_apply=%region_6.0 | all-reduce | flops 4 | bytes 32 | tf_op jit(solution)/shard_map/psum | solution.py:51
  142.1 31.8 %all-reduce.5.cloned.1.call-done = f32[2,4,128,128]{3,2,1,0:T(8,128)} async-done(((f32[2,4,128,128]{3,2,1,0:T(8,128)}), f32[2,4,128,128]{3,2,1,0:T(8,128)}) %all-reduce.5.cloned.1.call-update) | async-done | bytes 524304 | tf_op jit(solution)/shard_map/psum | solution.py:47
  173.9 1.2 multiply_reduce_fusion.1
  175.3 21.3 %psum.31 = f32[64]{0:T(128)S(1)} all-reduce(f32[64]{0:T(128)S(1)} %convolution_bitcast_fusion.2), channel_id=1, replica_groups=mesh['dp'=8,'expert'=2,'tensor'=2] {'dp'}, use_global_device_ids=true, to_apply=%region_7.0 | all-reduce | flops 64 | bytes 512 | tf_op jit(solution)/shard_map/psum | solution.py:60
  196.7 0.6 multiply_reduce_fusion.3
  198.0 0.6 multiply_reduce_fusion.2
  199.3 0.6 add_subtract_fusion
  (29 shorter events, 0.6 us)
Async XLA Ops:
  6.5 1.7 copy-start
  6.5 4.8 %copy-start.3 = (bf16[2,1792,128]{2,1,0:T(8,128)(2,1)S(1)}, bf16[2,1792,128]{2,1,0:T(8,128)(2,1)}, u32[]{:S(2)}) copy-start(bf16[2,1792,128]{2,1,0:T(8,128)(2,1)} %param.14) | copy-start | bytes 2752516
  6.5 70.6 %all-reduce.9.cloned.1.call-start = ((), (), s32[]{:S(2)}) async-start(), calls=%async_computation.4 | async-start | bytes 1048576
  11.3 84.6 %reduce-scatter.4.cloned.1.call-start = ((), (), s32[]{:S(2)}) async-start(), calls=%async_computation.3 | async-start | bytes 1572864
  43.2 29.4 %copy-start.9 = (u32[32]{0:T(128)S(1)}, u32[32]{0:T(128)}, u32[]{:S(2)}) copy-start(u32[32]{0:T(128)} %constant.29) | copy-start | bytes 388
  43.2 30.7 %copy-start.7 = (bf16[3584,128]{1,0:T(8,128)(2,1)S(1)}, bf16[3584,128]{1,0:T(8,128)(2,1)}, u32[]{:S(2)}) copy-start(bf16[3584,128]{1,0:T(8,128)(2,1)} %param.19) | copy-start | bytes 2752516
  72.6 65.7 %all-reduce.7.cloned.1.call-start = ((), (), s32[]{:S(2)}) async-start(), calls=%async_computation.2 | async-start | bytes 2097152 | tf_op jit(solution)/shard_map/psum | solution.py:49
  73.9 7.4 %copy-start.2 = (bf16[2,3584,128]{2,1,0:T(8,128)(2,1)S(1)}, bf16[2,3584,128]{2,1,0:T(8,128)(2,1)}, u32[]{:S(2)}) copy-start(bf16[2,3584,128]{2,1,0:T(8,128)(2,1)} %param.15) | copy-start | bytes 5505028
  81.0 92.9 %all-reduce.5.cloned.1.call-start = ((), (), s32[]{:S(2)}) async-start(), calls=%async_computation.1 | async-start | bytes 1048576 | tf_op jit(solution)/shard_map/psum | solution.py:47
  115.3 22.9 %copy-start.4 = (f32[4,128,128]{2,1,0:T(8,128)S(1)}, f32[4,128,128]{2,1,0:T(8,128)}, u32[]{:S(2)}) copy-start(f32[4,128,128]{2,1,0:T(8,128)} %param.21) | copy-start | bytes 786436
  115.3 58.6 %copy-start.5 = (f32[2,128,128]{2,1,0:T(8,128)S(1)}, f32[2,128,128]{2,1,0:T(8,128)}, u32[]{:S(2)}) copy-start(f32[2,128,128]{2,1,0:T(8,128)} %param.20) | copy-start | bytes 393220
  115.3 84.5 %copy-start.1 = (bf16[4,4,64,1280]{3,2,1,0:T(8,128)(2,1)S(1)}, bf16[4,4,64,1280]{3,2,1,0:T(8,128)(2,1)}, u32[]{:S(2)}) copy-start(bf16[4,4,64,1280]{3,2,1,0:T(8,128)(2,1)} %param.16) | copy-start | bytes 7864324
  128.5 46.6 %copy-start.8 = (s32[4]{0:T(128)S(1)}, s32[4]{0:T(128)}, u32[]{:S(2)}) copy-start(s32[4]{0:T(128)} %param.22) | copy-start | bytes 52
  128.5 69.5 %copy-start.6 = (f32[64]{0:T(128)S(1)}, f32[64]{0:T(128)}, u32[]{:S(2)}) copy-start(f32[64]{0:T(128)} %param.23) | copy-start | bytes 772
Sparse Core Ops, SparseCore 0:
  11.4 31.3 all-reduce.8
  72.7 23.1 reduce-scatter.3
  98.1 40.0 all-reduce.6
  140.5 33.4 all-reduce.4
where the time goes:
time: 207 us; the launch traced here: 206 us
  local copies, waits for them, and re-layouts  92.7 us (45%)
  waiting for transfers between devices  47.4 us (23%)
  blocking collectives  23.8 us (11%)
  matrix products  22.5 us (11%)
  between operations  15.3 us (7%)
  other arithmetic  4.44 us (2%)
    unnamed x25, local copies, waits for them, and re-layouts  78.4 us
    psum x1, waiting for transfers between devices, per_device(): dense_full = lax.psum(dense_portion, ('expert', 'tensor'))  31.8 us
    psum x1, blocking collectives, per_device(): domain_total = lax.psum(domain_part, 'dp')  21.3 us
    reduce_scatter x1, local copies, waits for them, and re-layouts, per_device(): lax.psum_scatter(jnp.einsum('lmtd,ldr->tlmr', block, dense_proj_in, prefe...  13.2 us
    unnamed x6, waiting for transfers between devices  8.98 us
    psum x1, waiting for transfers between devices, per_device(): expert_full = lax.psum(expert_part, 'tensor')  6.66 us
    dot_general x1, matrix products, per_device(): jnp.einsum('lmtd,ldr->tlmr', dense_cot, dense_proj_out, preferred_element...  5.64 us
    dot_general x1, matrix products, per_device(): jnp.einsum('lmtd,ldr->tlmr', block, dense_proj_in, preferred_element_type...  5.62 us
  transfers between devices with their start and end apart: 4, of which 3 were waited for; matrix products, arithmetic and copies ran while one was open for 54% of the time, Pallas kernels for 0%

commit v1 on v0

--- a/solution.py
+++ b/solution.py
@@ -57,7 +57,11 @@
     share_tally_count = domains // lax.axis_size("dp")
     first_domain = lax.axis_index("dp") * share_tally_count
     previous_domain_share = lax.dynamic_slice_in_dim(prior_mix, first_domain, share_tally_count, 0)
-    domain_total = lax.psum(domain_part, "dp")
+    domain_total = domain_part
+    for hop in (1, 2, 4):
+        domain_total = domain_total + lax.ppermute(
+            domain_total, "dp", [(dev, dev ^ hop) for dev in range(8)]
+        )
     spread = jnp.sqrt(jnp.mean(domain_total * domain_total) + 1e-06)
     z_value = domain_total / spread
     mass = jnp.sum(prior_mix * jnp.exp(0.5 * z_value))

time: 207 us -> 197 us (0.952)
  blocking collectives: 23.8 us -> 2.44 us
  waiting for transfers between devices: 47.4 us -> 53.6 us
  starting transfers between devices: 0.31 us -> 5.68 us
    psum x1 -> x0, blocking collectives: 21.3 us -> none  [per_device(): domain_total = lax.psum(domain_part, 'dp')]
    ppermute x0 -> x3, waiting for transfers between devices: none -> 6.24 us  [per_device(): lax.ppermute(domain_total, 'dp', [(dev, dev ^ hop) for dev in range(8)])]
    ppermute x0 -> x3, starting transfers between devices: none -> 5.38 us  [per_device(): lax.ppermute(domain_total, 'dp', [(dev, dev ^ hop) for dev in range(8)])]
  transfers between devices with their start and end apart: 4 -> 7, of which waited for: 3 -> 6; matrix products, arithmetic and copies ran while one was open for 54% -> 57% of each run, Pallas kernels for 0% -> 0%
where the time goes in v1:
time: 197 us
  local copies, waits for them, and re-layouts  92.7 us (47%)
  waiting for transfers between devices  53.6 us (27%)
  matrix products  22.5 us (11%)
  between operations  15.3 us (8%)
  starting transfers between devices  5.68 us (3%)
  other arithmetic  4.44 us (2%)
  blocking collectives  2.44 us (1%)
    unnamed x25, local copies, waits for them, and re-layouts  78.4 us
    psum x1, waiting for transfers between devices, per_device(): dense_full = lax.psum(dense_portion, ('expert', 'tensor'))  31.8 us
    reduce_scatter x1, local copies, waits for them, and re-layouts, per_device(): lax.psum_scatter(jnp.einsum('lmtd,ldr->tlmr', block, dense_proj_in, prefe...  13.2 us
    unnamed x6, waiting for transfers between devices  8.97 us
    psum x1, waiting for transfers between devices, per_device(): expert_full = lax.psum(expert_part, 'tensor')  6.64 us
    ppermute x3, waiting for transfers between devices, per_device(): lax.ppermute(domain_total, 'dp', [(dev, dev ^ hop) for dev in range(8)])  6.24 us
    dot_general x1, matrix products, per_device(): jnp.einsum('lmtd,ldr->tlmr', dense_cot, dense_proj_out, preferred_element...  5.64 us
    dot_general x1, matrix products, per_device(): jnp.einsum('lmtd,ldr->tlmr', block, dense_proj_in, preferred_element_type...  5.63 us
  transfers between devices with their start and end apart: 7, of which 6 were waited for; matrix products, arithmetic and copies ran while one was open for 57% of the time, Pallas kernels for 0%

profile of v1, /device:TPU:0, one launch (start us, length us, event | category | flops | bytes accessed | tf_op | source)
XLA Modules:
  0.0 196.7 jit_solution(17122013926873175403)
XLA Ops:
  6.5 1.7 copy-done
  8.3 1.8 convolution_bitcast_fusion.1
  10.1 1.1 copy.18
  11.3 5.6 %convolution_bitcast_fusion = f32[256,2,4,128]{0,3,2,1:T(8,128)S(1)} fusion(bf16[2,4,256,1792]{3,2,1,0:T(8,128)(2,1)} %param.12, bf16[2,1792,128]{2,1,0:T(8,128)(2,1)S(1)} %copy-done.3), kind=kOutput, calls=%fused_computation.2 | convolution fusion | flops 939524096 | bytes 9306112 | tf_op jit(solution)/shard_map/lmtd,ldr->tlmr/dot_general | solution.py:23
  17.0 26.2 %copy.29 = f32[256,2,4,128]{2,3,1,0:T(8,128)} copy(f32[256,2,4,128]{0,3,2,1:T(8,128)S(1)} %convolution_bitcast_fusion) | data formatting | bytes 2097152
  43.2 29.3 %reshape.9 = f32[256,1024]{1,0:T(8,128)} reshape(f32[256,2,128,4]{3,2,1,0:T(8,128)} %bitcast.46) | data formatting | bytes 2097152
  73.9 3.3 %fusion.6 = f32[128,4,4,32]{0,3,2,1:T(8,128)S(1)} fusion(bf16[4,4,32,3584]{3,2,1,0:T(8,128)(2,1)} %param.17, bf16[3584,128]{1,0:T(8,128)(2,1)S(1)} %copy-done.7), kind=kOutput, calls=%fused_computation.8 | convolution fusion | flops 469762048 | bytes 4849664 | tf_op jit(solution)/shard_map/mecd,dr->cmer/dot_general | solution.py:41
  78.2 2.8 %fusion.9 = f32[4,4,128,128]{3,2,1,0:T(8,128)} fusion(f32[128,4,4,32]{0,3,2,1:T(8,128)S(1)} %fusion.6, f32[32,4,4,128]{3,2,1,0:T(4,128)S(1)} %constant_dynamic-slice_fusion), kind=kOutput, calls=%fused_computation.12 | convolution fusion | flops 100663296 | bytes 1572864 | tf_op jit(solution)/shard_map/cmer,cmes->mers/dot_general | solution.py:44
  81.3 5.6 %fusion.2 = f32[128,2,4,128]{0,3,2,1:T(8,128)S(1)} fusion(bf16[2,4,128,3584]{3,2,1,0:T(8,128)(2,1)} %param.13, bf16[2,3584,128]{2,1,0:T(8,128)(2,1)S(1)} %copy-done.2), kind=kOutput, calls=%fused_computation.3 | convolution fusion | flops 939524096 | bytes 9699328 | tf_op jit(solution)/shard_map/lmtd,ldr->tlmr/dot_general | solution.py:28
  86.9 8.9 %reduce-scatter.4.cloned.1.call-done = f32[128,1024]{1,0:T(8,128)} async-done(((f32[256,1024]{1,0:T(8,128)}), f32[128,1024]{1,0:T(8,128)}) %reduce-scatter.4.cloned.1.call-update) | async-done | bytes 524304
  95.8 19.5 %reshape.10 = f32[128,2,128,4]{3,2,1,0:T(8,128)} reshape(f32[128,1024]{1,0:T(8,128)} %reduce-scatter.4.cloned.1.call-done) | data formatting | bytes 1048576
  115.3 13.2 %copy.16 = f32[128,2,4,128]{0,3,2,1:T(8,128)} copy(f32[128,2,4,128]{2,3,1,0:T(8,128)} %bitcast.47) | data formatting | bytes 1048576 | tf_op jit(solution)/shard_map/reduce_scatter | solution.py:22
  128.5 3.1 %fusion.12 = f32[2,4,128,128]{3,2,1,0:T(8,128)} fusion(f32[128,2,4,128]{0,3,2,1:T(8,128)} %copy.16, f32[128,2,4,128]{0,3,2,1:T(8,128)S(1)} %fusion.2), kind=kOutput, calls=%fused_computation.22 | convolution fusion | flops 201326592 | bytes 1572864 | tf_op jit(solution)/shard_map/fquy,fquh->quyh/dot_general | solution.py:31
  131.6 6.6 %all-reduce.7.cloned.1.call-done = f32[4,4,128,128]{3,2,1,0:T(8,128)} async-done(((f32[4,4,128,128]{3,2,1,0:T(8,128)}), f32[4,4,128,128]{3,2,1,0:T(8,128)}) %all-reduce.7.cloned.1.call-update) | async-done | bytes 1048592 | tf_op jit(solution)/shard_map/psum | solution.py:49
  138.3 1.4 multiply_reduce_fusion
  139.7 2.4 %psum.23 = f32[4]{0:T(128)S(1)} all-reduce(f32[4]{0:T(128)S(1)} %multiply_reduce_fusion), channel_id=1, replica_groups=mesh['dp'=8,'expert'=2,'tensor'=2] {'expert'}, use_global_device_ids=true, to_apply=%region_6.0 | all-reduce | flops 4 | bytes 32 | tf_op jit(solution)/shard_map/psum | solution.py:51
  142.1 31.8 %all-reduce.5.cloned.1.call-done = f32[2,4,128,128]{3,2,1,0:T(8,128)} async-done(((f32[2,4,128,128]{3,2,1,0:T(8,128)}), f32[2,4,128,128]{3,2,1,0:T(8,128)}) %all-reduce.5.cloned.1.call-update) | async-done | bytes 524304 | tf_op jit(solution)/shard_map/psum | solution.py:47
  173.9 1.2 multiply_reduce_fusion.1
  175.3 1.5 collective-permute-start
  176.8 2.1 %collective-permute-done = f32[64]{0:T(128)S(1)} collective-permute-done((f32[64]{0:T(128)S(1)}, f32[64]{0:T(128)S(1)}, u32[]{:S(2)}, u32[]{:S(2)}) %collective-permute-start) | collective-permute-done | bytes 288 | tf_op jit(solution)/shard_map/ppermute | solution.py:62
  178.9 1.5 collective-permute-start.1
  180.4 2.1 %collective-permute-done.1 = f32[64]{0:T(128)S(1)} collective-permute-done((f32[64]{0:T(128)S(1)}, f32[64]{0:T(128)S(1)}, u32[]{:S(2)}, u32[]{:S(2)}) %collective-permute-start.1) | collective-permute-done | bytes 288 | tf_op jit(solution)/shard_map/ppermute | solution.py:62
  182.5 2.4 %collective-permute-start.2 = (f32[64]{0:T(128)S(1)}, f32[64]{0:T(128)S(1)}, u32[]{:S(2)}, u32[]{:S(2)}) collective-permute-start(f32[64]{0:T(128)S(1)} %add.35), channel_id=1, source_target_pairs={{0,16},{4,20},{8,24},{12,28},{16,0},{20,4},{24,8},{28,12},{1,17},{... | collective-permute-start | bytes 776 | tf_op jit(solution)/shard_map/ppermute | solution.py:62
  184.9 2.1 %collective-permute-done.2 = f32[64]{0:T(128)S(1)} collective-permute-done((f32[64]{0:T(128)S(1)}, f32[64]{0:T(128)S(1)}, u32[]{:S(2)}, u32[]{:S(2)}) %collective-permute-start.2) | collective-permute-done | bytes 288 | tf_op jit(solution)/shard_map/ppermute | solution.py:62
  (36 shorter events, 4.0 us)
Async XLA Ops:
  6.5 1.7 copy-start
  6.5 4.8 %copy-start.3 = (bf16[2,1792,128]{2,1,0:T(8,128)(2,1)S(1)}, bf16[2,1792,128]{2,1,0:T(8,128)(2,1)}, u32[]{:S(2)}) copy-start(bf16[2,1792,128]{2,1,0:T(8,128)(2,1)} %param.14) | copy-start | bytes 2752516
  6.5 70.7 %all-reduce.9.cloned.1.call-start = ((), (), s32[]{:S(2)}) async-start(), calls=%async_computation.4 | async-start | bytes 1048576
  11.3 84.6 %reduce-scatter.4.cloned.1.call-start = ((), (), s32[]{:S(2)}) async-start(), calls=%async_computation.3 | async-start | bytes 1572864
  43.2 29.4 %copy-start.9 = (u32[32]{0:T(128)S(1)}, u32[32]{0:T(128)}, u32[]{:S(2)}) copy-start(u32[32]{0:T(128)} %constant.29) | copy-start | bytes 388
  43.2 30.7 %copy-start.7 = (bf16[3584,128]{1,0:T(8,128)(2,1)S(1)}, bf16[3584,128]{1,0:T(8,128)(2,1)}, u32[]{:S(2)}) copy-start(bf16[3584,128]{1,0:T(8,128)(2,1)} %param.19) | copy-start | bytes 2752516
  72.6 65.7 %all-reduce.7.cloned.1.call-start = ((), (), s32[]{:S(2)}) async-start(), calls=%async_computation.2 | async-start | bytes 2097152 | tf_op jit(solution)/shard_map/psum | solution.py:49
  73.9 7.4 %copy-start.2 = (bf16[2,3584,128]{2,1,0:T(8,128)(2,1)S(1)}, bf16[2,3584,128]{2,1,0:T(8,128)(2,1)}, u32[]{:S(2)}) copy-start(bf16[2,3584,128]{2,1,0:T(8,128)(2,1)} %param.15) | copy-start | bytes 5505028
  81.1 92.8 %all-reduce.5.cloned.1.call-start = ((), (), s32[]{:S(2)}) async-start(), calls=%async_computation.1 | async-start | bytes 1048576 | tf_op jit(solution)/shard_map/psum | solution.py:47
  115.3 22.9 %copy-start.4 = (f32[4,128,128]{2,1,0:T(8,128)S(1)}, f32[4,128,128]{2,1,0:T(8,128)}, u32[]{:S(2)}) copy-start(f32[4,128,128]{2,1,0:T(8,128)} %param.21) | copy-start | bytes 786436
  115.3 58.6 %copy-start.5 = (f32[2,128,128]{2,1,0:T(8,128)S(1)}, f32[2,128,128]{2,1,0:T(8,128)}, u32[]{:S(2)}) copy-start(f32[2,128,128]{2,1,0:T(8,128)} %param.20) | copy-start | bytes 393220
  115.3 74.8 %copy-start.1 = (bf16[4,4,64,1280]{3,2,1,0:T(8,128)(2,1)S(1)}, bf16[4,4,64,1280]{3,2,1,0:T(8,128)(2,1)}, u32[]{:S(2)}) copy-start(bf16[4,4,64,1280]{3,2,1,0:T(8,128)(2,1)} %param.16) | copy-start | bytes 7864324
  128.5 46.6 %copy-start.8 = (s32[4]{0:T(128)S(1)}, s32[4]{0:T(128)}, u32[]{:S(2)}) copy-start(s32[4]{0:T(128)} %param.22) | copy-start | bytes 52
  128.5 59.7 %copy-start.6 = (f32[64]{0:T(128)S(1)}, f32[64]{0:T(128)}, u32[]{:S(2)}) copy-start(f32[64]{0:T(128)} %param.23) | copy-start | bytes 772
  175.3 3.6 %collective-permute-start = (f32[64]{0:T(128)S(1)}, f32[64]{0:T(128)S(1)}, u32[]{:S(2)}, u32[]{:S(2)}) collective-permute-start(f32[64]{0:T(128)S(1)} %convolution_bitcast_fusion.2), channel_id=1, source_target_pairs={{0,4},{4,0},{8,12},{12,8},{16,20},{20,16},{24,28},{28,24},{1,5},{5... | collective-permute-start | bytes 776 | tf_op jit(solution)/shard_map/ppermute | solution.py:62
  178.9 3.6 %collective-permute-start.1 = (f32[64]{0:T(128)S(1)}, f32[64]{0:T(128)S(1)}, u32[]{:S(2)}, u32[]{:S(2)}) collective-permute-start(f32[64]{0:T(128)S(1)} %add.34), channel_id=1, source_target_pairs={{0,8},{4,12},{8,0},{12,4},{16,24},{20,28},{24,16},{28,20},{1,9},{5... | collective-permute-start | bytes 776 | tf_op jit(solution)/shard_map/ppermute | solution.py:62
  182.5 4.5 %collective-permute-start.2 = (f32[64]{0:T(128)S(1)}, f32[64]{0:T(128)S(1)}, u32[]{:S(2)}, u32[]{:S(2)}) collective-permute-start(f32[64]{0:T(128)S(1)} %add.35), channel_id=1, source_target_pairs={{0,16},{4,20},{8,24},{12,28},{16,0},{20,4},{24,8},{28,12},{1,17},{... | collective-permute-start | bytes 776 | tf_op jit(solution)/shard_map/ppermute | solution.py:62
Sparse Core Ops, SparseCore 0:
  11.4 31.3 all-reduce.8
  72.7 23.0 reduce-scatter.3
  98.1 40.0 all-reduce.6
  140.5 33.4 all-reduce.4
